TPU v7x, 32 devices: a whole 2x2x4 slice. The times are simulated.
32 devices in a mesh: dp: 4 (over y, x), fsdp: 8 (over z, core).
Axes of the slice: x: 2, y: 2, z: 4, core: 2. Of those that a mesh axis runs over, the one named last changes fastest.
Arguments:
- tokens: bfloat16 [96, 257, 1408], P(('dp', 'fsdp')), parts along dimension 0, may hold values from -16 to 16
- ln1_gain: float32 [1408], replicated, may hold values from 0.1 to 1.9
- ln1_bias: float32 [1408], replicated, may hold values from -3 to 3
- qkv_weight: bfloat16 [1408, 4224], P('fsdp'), may hold values from -3 to 3
- qkv_bias: float32 [4224], replicated, may hold values from -3 to 3
- proj_weight: bfloat16 [1408, 1408], P('fsdp'), may hold values from -0.15625 to 0.15625
- proj_bias: float32 [1408], replicated, may hold values from -3 to 3
- ln2_gain: float32 [1408], replicated, may hold values from 0.1 to 1.9
- ln2_bias: float32 [1408], replicated, may hold values from -3 to 3
- fc1_weight: bfloat16 [1408, 3072], P('fsdp'), may hold values from -0.15625 to 0.15625
- fc1_bias: float32 [3072], replicated, may hold values from -3 to 3
- fc2_weight: bfloat16 [3072, 1408], P('fsdp'), may hold values from -0.109375 to 0.109375
- fc2_bias: float32 [1408], replicated, may hold values from -3 to 3
Outputs:
- layer_out: bfloat16 [96, 257, 1408], P(('dp', 'fsdp')), parts along dimension 0
There are 4 independent parts, one for each index of `dp`. A program takes and returns all parts, laid end to end along the dimension named above; an argument that names none is the same for every part. Nothing has to cross between parts.
All inputs are finite; a program needn't handle non-finite values.
Results may differ from a plain program's by a relative error of at most 0.0045.
Values may be sent and summed in bfloat16 or wider, within the bound.
A program may use at most 448 MiB of HBM per device.

v0:
```python
import functools
import jax
import jax.numpy as jnp
from jax import lax
from jax.experimental import pallas as pl
from jax.experimental.pallas import tpu as pltpu
from jax.sharding import PartitionSpec as P

HEADS = 16


def layer_norm(values, gain, bias):
    average = jnp.mean(values, axis=-1, keepdims=True)
    centered = values - average
    variance = jnp.mean(centered * centered, axis=-1, keepdims=True)
    return centered * lax.rsqrt(variance + 1e-06) * gain + bias


def gather(block):
    return lax.all_gather(block, "fsdp", axis=0, tiled=True)


def gather_by_share(block):
    shares = lax.axis_size("dp")
    rows, columns = block.shape
    if shares & (shares - 1) or rows % (shares * 8):
        return None
    depth = rows // shares
    me = lax.axis_index("dp")
    share = lax.dynamic_slice_in_dim(block, me * depth, depth, 0)
    return gather(share).reshape(-1, depth, columns)


def exchange(share):
    shares = lax.axis_size("dp")
    me = lax.axis_index("dp")
    pieces = jnp.stack(
        [share]
        + [
            lax.ppermute(share, "dp", [(i, i ^ step) for i in range(shares)])
            for step in range(1, shares)
        ]
    )
    ordered = [
        lax.dynamic_index_in_dim(pieces, jnp.bitwise_xor(me, at), 0, keepdims=False)
        for at in range(shares)
    ]
    return jnp.stack(ordered, axis=1).reshape(-1, share.shape[2])


def after(block, earlier):
    return lax.optimization_barrier((block, earlier))


def product(left, weight):
    return jnp.dot(left, weight, preferred_element_type=jnp.float32)


def attend_kernel(head_size, q_ref, k_ref, v_ref, out_ref):
    scale = head_size ** (-0.5)
    for head in range(q_ref.shape[2] // head_size):
        at = slice(head * head_size, (head + 1) * head_size)
        scores = lax.dot_general(
            q_ref[0, :, at],
            k_ref[0, :, at],
            (((1,), (1,)), ((), ())),
            preferred_element_type=jnp.float32,
        )
        top = jnp.max(scores, axis=-1, keepdims=True)
        weights = jnp.exp((scores - top) * scale)
        probs = weights / jnp.sum(weights, axis=-1, keepdims=True)
        mixed = jnp.dot(
            probs.astype(jnp.bfloat16), v_ref[0, :, at], preferred_element_type=jnp.float32
        )
        out_ref[0, :, at] = mixed.astype(jnp.bfloat16)


def attend(qkv, head_size):
    images, seq_len, wide = qkv.shape
    width = wide // 3
    spec = [
        pl.BlockSpec((1, seq_len, width), functools.partial(lambda part, i: (i, 0, part), part))
        for part in range(3)
    ]
    return pl.pallas_call(
        functools.partial(attend_kernel, head_size),
        grid=(images,),
        in_specs=spec,
        out_specs=pl.BlockSpec((1, seq_len, width), lambda i: (i, 0, 0)),
        out_shape=jax.ShapeDtypeStruct((images, seq_len, width), jnp.bfloat16),
        compiler_params=pltpu.CompilerParams(vmem_limit_bytes=48 * 1024 * 1024),
        cost_estimate=pl.CostEstimate(
            flops=4 * images * seq_len * seq_len * width,
            bytes_accessed=8 * images * seq_len * width,
            transcendentals=images * seq_len * seq_len * width // head_size,
        ),
    )(qkv, qkv, qkv)


def on_device(
    tokens,
    ln1_gain,
    ln1_bias,
    qkv_weight,
    qkv_bias,
    proj_weight,
    proj_bias,
    ln2_gain,
    ln2_bias,
    fc1_weight,
    fc1_bias,
    fc2_weight,
    fc2_bias,
):
    images = tokens.shape[0]
    seq_len = tokens.shape[1]
    width = tokens.shape[2]
    head_count = HEADS
    head_size = width // head_count
    flat_rows = tokens.reshape(-1, width)
    resid_input = flat_rows.astype(jnp.float32)
    normed = layer_norm(resid_input, ln1_gain, ln1_bias).astype(jnp.bfloat16)
    row_count = normed.shape[0]
    fc2_share = gather_by_share(fc2_weight)
    fc1_weight, normed = after(fc1_weight, normed)
    qkv_sum = product(normed, gather(qkv_weight))
    qkv_proj = (qkv_sum + qkv_bias).astype(jnp.bfloat16).reshape(images, seq_len, 3 * width)
    if fc2_share is None:
        fc2_weight, qkv_proj = after(fc2_weight, qkv_proj)
        fc2_full = gather(fc2_weight)
    else:
        fc2_share, qkv_proj = after(fc2_share, qkv_proj)
        fc2_full = exchange(fc2_share)
    attended = attend(qkv_proj, head_size).reshape(row_count, width)
    projected = product(attended, gather(proj_weight))
    resid = projected + proj_bias + resid_input
    normed_two = layer_norm(resid, ln2_gain, ln2_bias).astype(jnp.bfloat16)
    fc2_full, normed_two = after(fc2_full, normed_two)
    pre_act = product(normed_two, gather(fc1_weight))
    hidden = jax.nn.gelu(pre_act + fc1_bias, approximate=False).astype(jnp.bfloat16)
    hidden = lax.optimization_barrier(hidden)
    down = product(hidden, fc2_full)
    result = down + fc2_bias + resid
    return result.astype(jnp.bfloat16).reshape(images, seq_len, width)


def solution(mesh):
    placed = (
        P(("dp", "fsdp"), None, None),
        P(),
        P(),
        P("fsdp", None),
        P(),
        P("fsdp", None),
        P(),
        P(),
        P(),
        P("fsdp", None),
        P(),
        P("fsdp", None),
        P(),
    )
    return jax.shard_map(
        on_device,
        mesh=mesh,
        in_specs=placed,
        out_specs=P(("dp", "fsdp"), None, None),
        check_vma=False,
    )
```

profile of v0, /device:TPU:0, one launch (start us, length us, event | category | flops | bytes accessed | tf_op | source)
XLA Modules:
  0.0 330.7 jit_solution(14583318338109750717)
XLA Ops:
  6.5 0.0 copy-start
  6.5 0.0 all-gather.7.cloned.1.call-start
  6.6 0.7 all-gather.7.cloned.1.call-update
  7.3 0.0 all-gather.5.cloned.1.call-start
  7.3 0.4 copy-done
  7.8 0.7 constant_dynamic-slice_fusion
  8.5 0.0 all-gather.5.cloned.1.call-update
  8.5 0.0 all-gather.9.cloned.1.call-start
  8.6 0.7 all-gather.9.cloned.1.call-update
  9.3 0.0 copy-start.11
  9.3 0.0 all-gather.11.cloned.1.call-start
  9.3 4.2 %reshape.79 = f32[771,1408]{1,0:T(8,128)} reshape(bf16[3,257,1408]{2,1,0:T(8,128)(2,1)} %param.13) | data formatting | bytes 6513408 | tf_op jit(solution)/shard_map/convert_element_type | solution.py:121
  13.5 0.0 copy-done.2
  13.5 0.4 convert_reduce_fusion
  14.0 0.1 div.15
  14.0 0.8 multiply_reduce_fusion
  14.8 0.1 rsqrt.20
  14.9 0.0 copy-done.7
  14.9 3.0 add_convert_fusion.3
  17.9 0.0 all-gather.11.cloned.1.call-update
  18.0 104.8 %all-gather.7.cloned.1.call-done = bf16[1408,4224]{1,0:T(8,128)(2,1)} async-done(((bf16[176,4224]{1,0:T(8,128)(2,1)}), bf16[1408,4224]{1,0:T(8,128)(2,1)}) %all-gather.7.cloned.1.call-update) | async-done | bytes 11894800 | tf_op jit(solution)/shard_map/all_gather | solution.py:20
  122.8 15.9 %add_convert_fusion = bf16[771,4224]{1,0:T(8,128)(2,1)} fusion(bf16[771,1408]{1,0:T(8,128)(2,1)S(1)} %add_convert_fusion.3, bf16[1408,4224]{1,0:T(8,128)(2,1)} %all-gather.7.cloned.1.call-done, f32[4224]{0:T(1024)S(1)} %copy-done.11), kind=kOutput, calls=%fused_computation.1 | convolution fusion | flops 9177391104 | bytes 20596224 | tf_op jit(solution)/shard_map/dot_general | solution.py:56
  138.7 7.3 %reshape.75.q_ref.k_ref.v_ref = bf16[3,257,4224]{2,1,0:T(8,128)(2,1)} reshape(bf16[771,4224]{1,0:T(8,128)(2,1)} %add_convert_fusion) | data formatting | bytes 13026816 | tf_op jit(solution)/shard_map/reshape | solution.py:127
  146.0 6.4 %all-gather.5.cloned.1.call-done = bf16[768,1408]{1,0:T(8,128)(2,1)} async-done(((bf16[96,1408]{1,0:T(8,128)(2,1)}), bf16[768,1408]{1,0:T(8,128)(2,1)}) %all-gather.5.cloned.1.call-update) | async-done | bytes 2162704 | tf_op jit(solution)/shard_map/all_gather | solution.py:20
  152.4 1.5 collective-permute-start
  153.8 1.5 collective-permute-start.1
  155.3 0.6 collective-permute-start.2
  155.9 37.4 %shard_map.127 = bf16[3,257,1408]{2,1,0:T(8,128)(2,1)S(1)} custom-call(bf16[3,257,4224]{2,1,0:T(8,128)(2,1)} %reshape.75.q_ref.k_ref.v_ref, bf16[3,257,4224]{2,1,0:T(8,128)(2,1)} %reshape.75.q_ref.k_ref.v_ref, bf16[3,257,4224]{2,1,0:T(8,128)(2,1)} %reshape.75.q_ref.k_ref.v_ref), custom_call_target="tpu_custom_call" | custom-call | flops 1115963904 | bytes 8684544 | tf_op jit(solution)/shard_map/pallas_call | solution.py:85
  193.3 1.9 reshape.77
  195.2 3.3 all-gather.9.cloned.1.call-done
  198.4 0.0 copy-done.13
  198.4 8.1 %fusion.10 = (f32[771]{0:T(1024)S(1)}, f32[771,1408]{1,0:T(8,128)S(1)}) fusion(f32[771,1408]{1,0:T(8,128)} %reshape.79, f32[1408]{0:T(1024)S(1)} %copy-done.13, bf16[771,1408]{1,0:T(8,128)(2,1)} %reshape.77, bf16[1408,1408]{1,0:T(8,128)(2,1)} %all-gather.9.cloned.1.call-done), kind=kOutput, calls=%fused_computation.38 | convolution fusion | flops 3060215040 | bytes 14829324 | tf_op jit(solution)/shard_map/dot_general | solution.py:56
  206.5 0.6 multiply_reduce_fusion.1
  207.2 2.1 add_convert_fusion.2
  209.3 0.0 collective-permute-done
  209.3 40.1 %collective-permute-done.1 = bf16[8,96,1408]{2,1,0:T(8,128)(2,1)} collective-permute-done((bf16[8,96,1408]{2,1,0:T(8,128)(2,1)}, bf16[8,96,1408]{2,1,0:T(8,128)(2,1)}, u32[]{:S(2)}, u32[]{:S(2)}) %collective-permute-start.1) | collective-permute-done | bytes 2162720 | tf_op jit(solution)/shard_map/ppermute | solution.py:40
  249.4 0.0 collective-permute-done.2
  249.4 0.0 copy-done.3
  249.4 4.0 %pad_maximum_fusion = bf16[4,8,96,1408]{3,2,1,0:T(8,128)(2,1)S(1)} fusion(bf16[1,8,96,1408]{3,2,1,0:T(8,128)(2,1)} %bitcast.4, bf16[1,8,96,1408]{3,2,1,0:T(8,128)(2,1)} %bitcast.3, bf16[1,8,96,1408]{3,2,1,0:T(8,128)(2,1)} %bitcast.2, bf16[1,8,96,1408]{3,2,1,0:T(8,128)(2,1)S(1)} %bitcast.26), kind=kLoop, calls=%fused_computation.20 | loop fusion | flops 12976128 | bytes 17301504 | tf_op jit(solution)/shard_map/stack | solution.py:37
  253.4 2.1 dynamic-slice_bitcast_fusion.3
  255.5 6.0 %pad_maximum_fusion.1 = bf16[8,4,96,1408]{3,2,1,0:T(8,128)(2,1)} fusion(bf16[8,1,96,1408]{3,2,1,0:T(8,128)(2,1)S(1)} %get-tuple-element.18, bf16[8,1,96,1408]{3,2,1,0:T(8,128)(2,1)S(1)} %get-tuple-element.19, bf16[8,1,96,1408]{3,2,1,0:T(8,128)(2,1)} %get-tuple-element.20, bf16[8,1,96,1408]{3,2,1,0:T(8,128)(2,1)S(1)} %get-tuple-element.17), kind=kLoop, calls=%fused_computation.21 | loop fusion | flops 12976128 | bytes 17301504 | tf_op jit(solution)/shard_map/stack | solution.py:48
  261.6 21.4 %all-gather.11.cloned.1.call-done = bf16[1408,3072]{1,0:T(8,128)(2,1)} async-done(((bf16[176,3072]{1,0:T(8,128)(2,1)}), bf16[1408,3072]{1,0:T(8,128)(2,1)}) %all-gather.11.cloned.1.call-update) | async-done | bytes 8650768 | tf_op jit(solution)/shard_map/all_gather | solution.py:20
  283.0 0.0 copy-done.5
  283.0 29.3 %fusion.2 = bf16[771,3072]{1,0:T(8,128)(2,1)S(1)} fusion(bf16[771,1408]{1,0:T(8,128)(2,1)S(1)} %copy-done.5, bf16[1408,3072]{1,0:T(8,128)(2,1)} %all-gather.11.cloned.1.call-done, f32[3072]{0:T(1024)S(1)} %copy-done.12), kind=kOutput, calls=%fused_computation.4 | convolution fusion | flops 6826051584 | bytes 15571200 | tf_op jit(solution)/shard_map/dot_general | solution.py:56
  312.3 0.0 copy-done.14
  312.3 0.0 copy-start.1
  312.3 9.9 %add_convert_fusion.1 = bf16[771,1408]{1,0:T(8,128)(2,1)S(1)} fusion(f32[771,1408]{1,0:T(8,128)} %copy-done.3, bf16[771,3072]{1,0:T(8,128)(2,1)S(1)} %fusion.2, bf16[3072,1408]{1,0:T(8,128)(2,1)S(1)} %bitcast.22, f32[1408]{0:T(1024)S(1)} %copy-done.14), kind=kOutput, calls=%fused_computation.23 | convolution fusion | flops 6672986112 | bytes 19906816 | tf_op jit(solution)/shard_map/dot_general | solution.py:56
  322.2 1.9 reshape.78
  (24 shorter events, 0.1 us)
Async XLA Ops:
  6.5 1.2 copy-start
  6.5 7.0 %copy-start.2 = (bf16[3,257,1408]{2,1,0:T(8,128)(2,1)S(1)}, bf16[3,257,1408]{2,1,0:T(8,128)(2,1)}, u32[]{:S(2)}) copy-start(bf16[3,257,1408]{2,1,0:T(8,128)(2,1)} %param.13) | copy-start | bytes 6513412
  6.5 8.4 %copy-start.8 = (f32[1408]{0:T(1024)S(1)}, f32[1408]{0:T(1024)}, u32[]{:S(2)}) copy-start(f32[1408]{0:T(1024)} %param.14) | copy-start | bytes 16900
  6.5 8.4 %copy-start.7 = (f32[1408]{0:T(1024)S(1)}, f32[1408]{0:T(1024)}, u32[]{:S(2)}) copy-start(f32[1408]{0:T(1024)} %param.15) | copy-start | bytes 16900
  6.5 116.2 %all-gather.7.cloned.1.call-start = ((), (), s32[]{:S(2)}) async-start(), calls=%async_computation.1 | async-start | bytes 13381632 | tf_op jit(solution)/shard_map/all_gather | solution.py:20
  7.3 145.1 %all-gather.5.cloned.1.call-start = ((), (), s32[]{:S(2)}) async-start(), calls=%async_computation | async-start | bytes 2433024 | tf_op jit(solution)/shard_map/all_gather | solution.py:20
  8.5 189.9 %all-gather.9.cloned.1.call-start = ((), (), s32[]{:S(2)}) async-start(), calls=%async_computation.2 | async-start | bytes 4460544 | tf_op jit(solution)/shard_map/all_gather | solution.py:20
  9.3 113.5 %copy-start.11 = (f32[4224]{0:T(1024)S(1)}, f32[4224]{0:T(1024)}, u32[]{:S(2)}) copy-start(f32[4224]{0:T(1024)} %param.17) | copy-start | bytes 50692
  9.3 273.7 %all-gather.11.cloned.1.call-start = ((), (), s32[]{:S(2)}) async-start(), calls=%async_computation.3 | async-start | bytes 9732096 | tf_op jit(solution)/shard_map/all_gather | solution.py:20
  152.4 46.0 %copy-start.13 = (f32[1408]{0:T(1024)S(1)}, f32[1408]{0:T(1024)}, u32[]{:S(2)}) copy-start(f32[1408]{0:T(1024)} %param.19) | copy-start | bytes 16900
  152.4 56.9 %collective-permute-start = (bf16[8,96,1408]{2,1,0:T(8,128)(2,1)}, bf16[8,96,1408]{2,1,0:T(8,128)(2,1)}, u32[]{:S(2)}, u32[]{:S(2)}) collective-permute-start(bf16[8,96,1408]{2,1,0:T(8,128)(2,1)} %bitcast.23), channel_id=1, source_target_pairs={{0,8},{8,0},{16,24},{24,16},{1,9},{9,1},{17,25},{25,17},{2,10},{10... | collective-permute-start | bytes 6488072 | tf_op jit(solution)/shard_map/ppermute | solution.py:40
  153.8 95.5 %collective-permute-start.1 = (bf16[8,96,1408]{2,1,0:T(8,128)(2,1)}, bf16[8,96,1408]{2,1,0:T(8,128)(2,1)}, u32[]{:S(2)}, u32[]{:S(2)}) collective-permute-start(bf16[8,96,1408]{2,1,0:T(8,128)(2,1)} %bitcast.24), channel_id=1, source_target_pairs={{0,16},{8,24},{16,0},{24,8},{1,17},{9,25},{17,1},{25,9},{2,18},{10... | collective-permute-start | bytes 6488072 | tf_op jit(solution)/shard_map/ppermute | solution.py:40
  155.3 94.1 %collective-permute-start.2 = (bf16[8,96,1408]{2,1,0:T(8,128)(2,1)}, bf16[8,96,1408]{2,1,0:T(8,128)(2,1)}, u32[]{:S(2)}, u32[]{:S(2)}) collective-permute-start(bf16[8,96,1408]{2,1,0:T(8,128)(2,1)} %bitcast.25), channel_id=1, source_target_pairs={{0,24},{8,16},{16,8},{24,0},{1,25},{9,17},{17,9},{25,1},{2,26},{10... | collective-permute-start | bytes 6488072 | tf_op jit(solution)/shard_map/ppermute | solution.py:40
  195.2 12.0 %copy-start.9 = (f32[1408]{0:T(1024)S(1)}, f32[1408]{0:T(1024)}, u32[]{:S(2)}) copy-start(f32[1408]{0:T(1024)} %param.21) | copy-start | bytes 16900
  195.2 12.0 %copy-start.10 = (f32[1408]{0:T(1024)S(1)}, f32[1408]{0:T(1024)}, u32[]{:S(2)}) copy-start(f32[1408]{0:T(1024)} %param.20) | copy-start | bytes 16900
  206.5 42.9 %copy-start.3 = (f32[771,1408]{1,0:T(8,128)}, f32[771,1408]{1,0:T(8,128)S(1)}, u32[]{:S(2)}) copy-start(f32[771,1408]{1,0:T(8,128)S(1)} %get-tuple-element.22) | copy-start | bytes 13026820
  206.5 42.9 %copy-start.6 = (bf16[768,1408]{1,0:T(8,128)(2,1)S(1)}, bf16[768,1408]{1,0:T(8,128)(2,1)}, u32[]{:S(2)}) copy-start(bf16[768,1408]{1,0:T(8,128)(2,1)} %all-gather.5.cloned.1.call-done) | copy-start | bytes 6488068
  255.5 27.5 %copy-start.5 = (bf16[771,1408]{1,0:T(8,128)(2,1)S(1)}, bf16[771,1408]{1,0:T(8,128)(2,1)}, u32[]{:S(2)}) copy-start(bf16[771,1408]{1,0:T(8,128)(2,1)} %add_convert_fusion.2) | copy-start | bytes 6513412
  255.5 27.5 %copy-start.12 = (f32[3072]{0:T(1024)S(1)}, f32[3072]{0:T(1024)}, u32[]{:S(2)}) copy-start(f32[3072]{0:T(1024)} %param.23) | copy-start | bytes 36868
  261.6 50.7 %copy-start.14 = (f32[1408]{0:T(1024)S(1)}, f32[1408]{0:T(1024)}, u32[]{:S(2)}) copy-start(f32[1408]{0:T(1024)} %param.25) | copy-start | bytes 16900
  283.0 29.3 %copy-start.4 = (bf16[8,4,96,1408]{3,2,1,0:T(8,128)(2,1)S(1)}, bf16[8,4,96,1408]{3,2,1,0:T(8,128)(2,1)}, u32[]{:S(2)}) copy-start(bf16[8,4,96,1408]{3,2,1,0:T(8,128)(2,1)} %pad_maximum_fusion.1) | copy-start | bytes 25952260
  312.3 11.8 %copy-start.1 = (bf16[384,1408]{1,0:T(8,128)(2,1)S(1)}, bf16[384,1408]{1,0:T(8,128)(2,1)}, u32[]{:S(2)}) copy-start(bf16[384,1408]{1,0:T(8,128)(2,1)} %param.24) | copy-start | bytes 3244036
Sparse Core Ops, SparseCore 0:
  9.0 113.7 all-gather.6
  124.4 27.9 all-gather.4
  154.0 44.3 all-gather.8
  199.9 83.0 all-gather.10
where the time goes:
time: 331 us
  waiting for transfers between devices  177 us (53%)
  matrix products  63.2 us (19%)
  Pallas kernels  37.4 us (11%)
  local copies, waits for them, and re-layouts  18.8 us (6%)
  other arithmetic  17 us (5%)
  between operations  13.3 us (4%)
  starting transfers between devices  3.64 us (1%)
    all_gather x4, waiting for transfers between devices, gather(): return lax.all_gather(block, 'fsdp', axis=0, tiled=True)  136 us
    dot_general x4, matrix products, product(): return jnp.dot(left, weight, preferred_element_type=jnp.float32)  63.2 us
    ppermute x3, waiting for transfers between devices, exchange(): lax.ppermute(share, 'dp', [(i, i ^ step) for i in range(shares)])  40.1 us
    pallas_call x1, Pallas kernels, attend(): pl.pallas_call(functools.partial(attend_kernel, head_size), grid=(images,...  37.4 us
    reshape x1, local copies, waits for them, and re-layouts, on_device(): (qkv_sum + qkv_bias).astype(jnp.bfloat16)  7.3 us
  transfers between devices with their start and end apart: 7, of which 5 were waited for; matrix products, arithmetic and copies ran while one was open for 17% of the time, Pallas kernels for 11%

commit v1 on v0

v1 whole, which is shorter than its diff:
```python
import functools
import math
import jax
import jax.numpy as jnp
from jax import lax
from jax.experimental import pallas as pl
from jax.experimental.pallas import tpu as pltpu
from jax.sharding import PartitionSpec as P

HEADS = 16
LANES = 128
PACK = 16
EPS = 1e-06


def layer_norm(values, gain, bias):
    average = jnp.mean(values, axis=-1, keepdims=True)
    centered = values - average
    variance = jnp.mean(centered * centered, axis=-1, keepdims=True)
    return centered * lax.rsqrt(variance + EPS) * gain + bias


def product(left, weight):
    return jnp.dot(left, weight, preferred_element_type=jnp.float32)


def round_up(value, step):
    return -(-value // step) * step


def row_block(rows, most):
    best = PACK
    for size in range(PACK, most + 1, PACK):
        if rows % size == 0:
            best = size
    return best


class Plan:
    def __init__(self, shares, ring, tokens, weights):
        self.shares, self.ring = shares, ring
        self.images, self.seq, self.width = tokens.shape
        qkv, proj, fc1, fc2 = weights
        self.depth = qkv.shape[0]
        self.deep = fc2.shape[0]
        self.wide = [w.shape[1] for w in (qkv, proj, fc1)]
        self.total = sum(self.wide)
        self.chunk = shares * LANES
        self.hidden = fc1.shape[1]
        self.seq_pad = round_up(self.seq, PACK)
        self.rows = self.images * self.seq_pad
        self.fits = (
            shares == 4
            and ring % 2 == 0
            and ring >= 4
            and self.depth % PACK == 0
            and self.depth >= 2 * PACK
            and self.deep % (shares * PACK) == 0
            and self.deep // shares >= 2 * PACK
            and all(w % LANES == 0 for w in self.wide)
            and self.total % self.chunk == 0
            and self.width % LANES == 0
        )
        if not self.fits:
            return
        self.narrow = 2 * LANES
        self.col_chunks = self.total // self.chunk
        self.kinds = [("col", 0, self.col_chunks, self.chunk, 0)]
        whole = self.width // self.narrow
        at = self.col_chunks
        self.kinds.append(("row", at, at + whole, self.narrow, 0))
        at += whole
        if self.width % self.narrow:
            self.kinds.append(("row", at, at + 1, self.width % self.narrow, whole * self.narrow))
            at += 1
        self.chunks = at
        kept = ring * (self.depth * self.total + self.deep * self.width) * 2
        acts = self.rows * (self.width * (4 + 2 + 2 + 2) + max(3 * self.width, self.hidden) * 2)
        self.fits = kept + acts < 58 * 1024 * 1024


def fused_kernel(plan, tokens, qkv_hbm, proj_hbm, fc1_hbm, fc2_hbm,
                 ln1_gain, ln1_bias, qkv_bias, proj_bias, ln2_gain, ln2_bias, fc1_bias, fc2_bias,
                 out, wall, wtwo, tok, resid, normed, qkv, mixed,
                 send_sem, recv_sem, own_sem, out_sem):
    shares, ring = plan.shares, plan.ring
    zs = ring // 2
    depth, deep = plan.depth, plan.deep
    rows, seq, seq_pad = plan.rows, plan.seq, plan.seq_pad
    share = lax.axis_index("dp")
    place = lax.axis_index("fsdp")
    z, core = place // 2, place % 2
    Z, X1, Y1, X2, Y2, PART = range(6)
    side_x = lax.rem(share, 2) * -2 + 1 + share
    side_y = share + 2 - (share // 2) * 4
    partner = z * 2 + 1 - core

    def others():
        for step in range(1, zs):
            yield lax.rem(z + step, zs)

    def device(d, f):
        return {"dp": d, "fsdp": f}

    def part(kind, who, block_share, low, high):
        name, first, _, cols, base = kind[:5]
        g = kind[5]
        if name == "col":
            r = pl.multiple_of(who * depth + low, PACK)
            c = pl.multiple_of((g * shares + block_share) * LANES, LANES)
            return wall.at[pl.ds(r, high - low), pl.ds(c, LANES)]
        size = deep // shares
        r = pl.multiple_of(who * deep + block_share * size + low, PACK)
        c = pl.multiple_of(base + (g - first) * cols, LANES)
        return wtwo.at[pl.ds(r, high - low), pl.ds(c, cols)]

    def entire(kind, who):
        name, first, _, cols, base = kind[:5]
        g = kind[5]
        if name == "col":
            return wall.at[pl.ds(pl.multiple_of(who * depth, PACK), depth),
                           pl.ds(pl.multiple_of(g * cols, LANES), cols)]
        return wtwo.at[pl.ds(pl.multiple_of(who * deep, PACK), deep),
                       pl.ds(pl.multiple_of(base + (g - first) * cols, LANES), cols)]

    def sized(kind, count, part_rows, cols):
        ref = wall if kind[0] == "col" else wtwo
        return ref.at[pl.ds(0, count * part_rows), pl.ds(0, cols)]

    def spans(kind):
        size = depth if kind[0] == "col" else deep // shares
        cut = round_up(size // 2, PACK)
        return size, cut, LANES if kind[0] == "col" else kind[3]

    def copy(ref, phase, g, d, f):
        return pltpu.make_async_remote_copy(
            src_ref=ref, dst_ref=ref, send_sem=send_sem.at[phase, g], recv_sem=recv_sem.at[phase, g],
            device_id=device(d, f), device_id_type=pl.DeviceIdType.MESH)

    def volume(kind, phase):
        size, cut, cols = spans(kind)
        if phase == PART:
            full = depth if kind[0] == "col" else deep
            return sized(kind, zs, full, kind[3])
        part_rows = {Z: size, X1: size, Y1: size, X2: cut, Y2: size - cut}[phase]
        return sized(kind, zs - 1, part_rows, cols)

    def wait_in(kind, phase):
        g = kind[5]
        pltpu.make_async_copy(volume(kind, phase), volume(kind, phase), recv_sem.at[phase, g]).wait()

    def wait_out(kind, phase):
        g = kind[5]
        pltpu.make_async_copy(volume(kind, phase), volume(kind, phase), send_sem.at[phase, g]).wait()

    def each_kind(g, body):
        if isinstance(g, int):
            for kind in plan.kinds:
                if kind[1] <= g < kind[2]:
                    body(kind + (g,))
            return
        for kind in plan.kinds:
            @pl.when(jnp.logical_and(g >= kind[1], g < kind[2]))
            def _(kind=kind):
                body(kind + (g,))

    def send_z(g):
        def body(kind):
            size, _, _ = spans(kind)
            for other in others():
                copy(part(kind, place, share, 0, size), Z, g, share, other * 2 + core).start()
        each_kind(g, body)

    def relay_a(g):
        def body(kind):
            size, _, _ = spans(kind)
            wait_in(kind, Z)
            for other in others():
                block = part(kind, other * 2 + core, share, 0, size)
                copy(block, X1, g, side_x, place).start()
                copy(block, Y1, g, side_y, place).start()
        each_kind(g, body)

    def relay_b(g):
        def body(kind):
            size, cut, _ = spans(kind)
            wait_in(kind, X1)
            wait_in(kind, Y1)
            for other in others():
                who = other * 2 + core
                copy(part(kind, who, side_y, 0, cut), X2, g, side_x, place).start()
                copy(part(kind, who, side_x, cut, size), Y2, g, side_y, place).start()
        each_kind(g, body)

    def relay_c(g):
        def body(kind):
            wait_in(kind, X2)
            wait_in(kind, Y2)
            for who in range(zs):
                copy(entire(kind, who * 2 + core), PART, g, share, partner).start()
        each_kind(g, body)

    def finish(g):
        each_kind(g, lambda kind: wait_in(kind, PART))

    ahead = 4

    def tick(t):
        if isinstance(t, int):
            for low, action in ((ahead, send_z), (0, relay_a), (-1, relay_b), (-2, relay_c)):
                if 0 <= t + low < plan.chunks:
                    action(t + low)
            return
        send_z(t + ahead)
        relay_a(t)
        relay_b(t - 1)
        relay_c(t - 2)

    token_copy = pltpu.make_async_copy(tokens, tok, own_sem.at[4])
    token_copy.start()
    base = 0
    own = []
    for at, (ref, cols) in enumerate(zip((qkv_hbm, proj_hbm, fc1_hbm), plan.wide)):
        own.append(pltpu.make_async_copy(
            ref, wall.at[pl.ds(pl.multiple_of(place * depth, PACK), depth), pl.ds(base, cols)], own_sem.at[at]))
        base += cols
    own.append(pltpu.make_async_copy(
        fc2_hbm, wtwo.at[pl.ds(pl.multiple_of(place * deep, PACK), deep), :], own_sem.at[3]))
    for c in own:
        c.start()

    barrier = pltpu.get_barrier_semaphore()
    peers = [(share, other * 2 + core) for other in others()]
    peers += [(side_x, place), (side_y, place), (share, partner)]
    for d, f in peers:
        pl.semaphore_signal(barrier, inc=1, device_id=device(d, f), device_id_type=pl.DeviceIdType.MESH)
    pl.semaphore_wait(barrier, len(peers))
    for c in own:
        c.wait()
    for g in range(ahead):
        send_z(g)

    token_copy.wait()
    resid[...] = jnp.zeros_like(resid)
    for i in range(plan.images):
        resid[pl.ds(i * seq_pad, seq), :] = tok[i].astype(jnp.float32)
    block = row_block(rows, 64)

    def norm(gain, bias):
        def body(r, carry):
            at = pl.ds(pl.multiple_of(r * block, PACK), block)
            normed[at, :] = layer_norm(resid[at, :], gain[...], bias[...]).astype(jnp.bfloat16)
            return carry
        lax.fori_loop(0, rows // block, body, 0)

    norm(ln1_gain, ln1_bias)

    qkv_cols = plan.wide[0]
    cols = plan.chunk

    def project(k, step):
        at = pl.ds(pl.multiple_of(k * cols, LANES), step)
        qkv[:, at] = (product(normed[...], wall[:, at]) + qkv_bias[:, at]).astype(jnp.bfloat16)

    t = 3
    for early in range(t):
        tick(early)
    whole = qkv_cols // cols

    def qkv_step(k, carry):
        tick(k + t)
        finish(k)
        project(k, cols)
        return carry

    lax.fori_loop(0, whole, qkv_step, 0)
    t += whole
    done = whole
    if qkv_cols % cols:
        tick(t)
        finish(done)
        project(whole, qkv_cols % cols)
        t += 1
        done += 1

    head_size = plan.width // HEADS
    scale = head_size ** (-0.5) * math.log2(math.e)
    width = plan.width
    per_image = 2

    def attend(i, carry):
        at = pl.ds(pl.multiple_of(i * seq_pad, PACK), seq_pad)
        some = pl.ds(pl.multiple_of(i * seq_pad, PACK), seq)
        for head in range(HEADS):
            low = head * head_size
            q = qkv[at, low:low + head_size]
            k = qkv[some, width + low:width + low + head_size]
            v = qkv[some, 2 * width + low:2 * width + low + head_size]
            scores = lax.dot_general(q, k, (((1,), (1,)), ((), ())), preferred_element_type=jnp.float32)
            top = jnp.max(scores, axis=-1, keepdims=True)
            weights = jnp.exp2((scores - top) * scale)
            norm_by = 1.0 / jnp.sum(weights, axis=-1, keepdims=True)
            mixed[at, low:low + head_size] = (
                product(weights.astype(jnp.bfloat16), v) * norm_by).astype(jnp.bfloat16)
            if (head + 1) % (HEADS // per_image) == 0:
                tick(t + i * per_image + (head + 1) // (HEADS // per_image) - 1)
        return carry

    lax.fori_loop(0, plan.images, attend, 0)
    t += plan.images * per_image

    proj_last = -(-(plan.wide[0] + plan.wide[1]) // cols)
    while done < proj_last:
        while t < done + 3:
            tick(t)
            t += 1
        finish(done)
        done += 1
    at_proj = plan.wide[0]
    for low in range(0, width, 2 * LANES):
        high = min(low + 2 * LANES, width)
        resid[:, low:high] = (product(mixed[...], wall[:, at_proj + low:at_proj + high])
                              + proj_bias[:, low:high] + resid[:, low:high])
    norm(ln2_gain, ln2_bias)

    at_fc1 = plan.wide[0] + plan.wide[1]
    low = 0
    begun = done * cols - at_fc1
    pieces = []
    if begun:
        pieces.append((0, begun, None))
    at = begun
    for g in range(done, plan.col_chunks):
        pieces.append((at, at + cols, g))
        at += cols

    def up(low, high):
        pre = product(normed[...], wall[:, at_fc1 + low:at_fc1 + high]) + fc1_bias[:, low:high]
        qkv[:, low:high] = (pre * (1.0 + lax.erf(pre * math.sqrt(0.5))) * 0.5).astype(jnp.bfloat16)

    for count, (low, high, g) in enumerate(pieces):
        if g is not None:
            if count % 2 == 0 or t < g + 3:
                tick(t)
                t += 1
            while t < g + 3:
                tick(t)
                t += 1
            finish(g)
        up(low, high)

    hidden = plan.hidden
    writes = []
    for g in range(plan.col_chunks, plan.chunks):
        while t < g + 3 or (g == plan.chunks - 1 and t < plan.chunks + 2):
            tick(t)
            t += 1
        finish(g)
        for kind in plan.kinds:
            if kind[1] <= g < kind[2]:
                low = kind[4] + (g - kind[1]) * kind[3]
                high = low + kind[3]
        down = product(qkv[:, :hidden], wtwo[:, low:high]) + fc2_bias[:, low:high] + resid[:, low:high]
        down = down.astype(jnp.bfloat16)
        for i in range(plan.images):
            tok[i, :, low:high] = down[i * seq_pad:i * seq_pad + seq]
            write = pltpu.make_async_copy(
                tok.at[i, :, pl.ds(low, high - low)], out.at[i, :, pl.ds(low, high - low)],
                out_sem.at[g - plan.col_chunks, i])
            write.start()
            writes.append(write)
    for write in writes:
        write.wait()
    for phase in (Z, X1, Y1, X2, Y2, PART):
        def drain(g, carry, phase=phase):
            each_kind(g, lambda kind: wait_out(kind, phase))
            return carry
        lax.fori_loop(0, plan.chunks, drain, 0)


def fused(plan, tokens, weights, vectors):
    vmem = pl.BlockSpec(memory_space=pltpu.VMEM)
    anywhere = pl.BlockSpec(memory_space=pl.ANY)
    count = plan.chunks
    inner = max(plan.wide[0], plan.hidden)
    return pl.pallas_call(
        functools.partial(fused_kernel, plan),
        out_shape=jax.ShapeDtypeStruct(tokens.shape, jnp.bfloat16),
        in_specs=[anywhere] * 5 + [vmem] * len(vectors),
        out_specs=anywhere,
        scratch_shapes=[
            pltpu.VMEM((plan.ring * plan.depth, plan.total), jnp.bfloat16),
            pltpu.VMEM((plan.ring * plan.deep, plan.width), jnp.bfloat16),
            pltpu.VMEM(tokens.shape, jnp.bfloat16),
            pltpu.VMEM((plan.rows, plan.width), jnp.float32),
            pltpu.VMEM((plan.rows, plan.width), jnp.bfloat16),
            pltpu.VMEM((plan.rows, inner), jnp.bfloat16),
            pltpu.VMEM((plan.rows, plan.width), jnp.bfloat16),
            pltpu.SemaphoreType.DMA((6, count)),
            pltpu.SemaphoreType.DMA((6, count)),
            pltpu.SemaphoreType.DMA((5,)),
            pltpu.SemaphoreType.DMA((count - plan.col_chunks, plan.images)),
        ],
        compiler_params=pltpu.CompilerParams(
            collective_id=0, has_side_effects=True, vmem_limit_bytes=67_043_328),
    )(tokens, *weights, *vectors)


def gather(block):
    return lax.all_gather(block, "fsdp", axis=0, tiled=True)


def attend_kernel(head_size, q_ref, k_ref, v_ref, out_ref):
    scale = head_size ** (-0.5)
    for head in range(q_ref.shape[2] // head_size):
        at = slice(head * head_size, (head + 1) * head_size)
        scores = lax.dot_general(
            q_ref[0, :, at], k_ref[0, :, at], (((1,), (1,)), ((), ())),
            preferred_element_type=jnp.float32)
        top = jnp.max(scores, axis=-1, keepdims=True)
        weights = jnp.exp((scores - top) * scale)
        probs = weights / jnp.sum(weights, axis=-1, keepdims=True)
        mixed = product(probs.astype(jnp.bfloat16), v_ref[0, :, at])
        out_ref[0, :, at] = mixed.astype(jnp.bfloat16)


def attend(qkv, head_size):
    images, seq_len, wide = qkv.shape
    width = wide // 3
    spec = [
        pl.BlockSpec((1, seq_len, width), functools.partial(lambda part, i: (i, 0, part), part))
        for part in range(3)
    ]
    return pl.pallas_call(
        functools.partial(attend_kernel, head_size),
        grid=(images,),
        in_specs=spec,
        out_specs=pl.BlockSpec((1, seq_len, width), lambda i: (i, 0, 0)),
        out_shape=jax.ShapeDtypeStruct((images, seq_len, width), jnp.bfloat16),
        compiler_params=pltpu.CompilerParams(vmem_limit_bytes=48 * 1024 * 1024),
        cost_estimate=pl.CostEstimate(
            flops=4 * images * seq_len * seq_len * width,
            bytes_accessed=8 * images * seq_len * width,
            transcendentals=images * seq_len * seq_len * width // head_size,
        ),
    )(qkv, qkv, qkv)


def plain(tokens, ln1_gain, ln1_bias, qkv_weight, qkv_bias, proj_weight, proj_bias,
          ln2_gain, ln2_bias, fc1_weight, fc1_bias, fc2_weight, fc2_bias):
    images, seq_len, width = tokens.shape
    resid_input = tokens.reshape(-1, width).astype(jnp.float32)
    normed = layer_norm(resid_input, ln1_gain, ln1_bias).astype(jnp.bfloat16)
    qkv_sum = product(normed, gather(qkv_weight))
    qkv_proj = (qkv_sum + qkv_bias).astype(jnp.bfloat16).reshape(images, seq_len, 3 * width)
    attended = attend(qkv_proj, width // HEADS).reshape(-1, width)
    resid = product(attended, gather(proj_weight)) + proj_bias + resid_input
    normed_two = layer_norm(resid, ln2_gain, ln2_bias).astype(jnp.bfloat16)
    pre_act = product(normed_two, gather(fc1_weight))
    hidden = jax.nn.gelu(pre_act + fc1_bias, approximate=False).astype(jnp.bfloat16)
    result = product(hidden, gather(fc2_weight)) + fc2_bias + resid
    return result.astype(jnp.bfloat16).reshape(images, seq_len, width)


def on_device(tokens, ln1_gain, ln1_bias, qkv_weight, qkv_bias, proj_weight, proj_bias,
              ln2_gain, ln2_bias, fc1_weight, fc1_bias, fc2_weight, fc2_bias):
    weights = (qkv_weight, proj_weight, fc1_weight, fc2_weight)
    plan = Plan(lax.axis_size("dp"), lax.axis_size("fsdp"), tokens, weights)
    if not plan.fits:
        return plain(tokens, ln1_gain, ln1_bias, qkv_weight, qkv_bias, proj_weight, proj_bias,
                     ln2_gain, ln2_bias, fc1_weight, fc1_bias, fc2_weight, fc2_bias)
    vectors = (ln1_gain, ln1_bias, qkv_bias, proj_bias, ln2_gain, ln2_bias, fc1_bias, fc2_bias)
    return fused(plan, tokens, weights, [v.reshape(1, -1) for v in vectors])


def solution(mesh):
    whole, rows = P(), P("fsdp", None)
    split = P(("dp", "fsdp"), None, None)
    placed = (split, whole, whole, rows, whole, rows, whole, whole, whole, rows, whole, rows, whole)
    return jax.shard_map(on_device, mesh=mesh, in_specs=placed, out_specs=split, check_vma=False)
```

time: 331 us -> 165 us (0.50)
  waiting for transfers between devices: 177 us -> 0 us
  Pallas kernels: 37.4 us -> 151 us
  matrix products: 63.2 us -> 0 us
  other arithmetic: 17 us -> 0 us
  between operations: 13.3 us -> 0.01 us
  local copies, waits for them, and re-layouts: 18.8 us -> 12.3 us
  starting transfers between devices: 3.64 us -> 0 us
    all_gather x4 -> x0, waiting for transfers between devices: 136 us -> none  [gather(): return lax.all_gather(block, 'fsdp', axis=0, tiled=True)]
    pallas_call x1, Pallas kernels: 37.4 us -> 151 us  [fused(): pl.pallas_call(functools.partial(fused_kernel, plan), out_shape=jax.Shape...]
    dot_general x4 -> x0, matrix products: 63.2 us -> none  [product(): return jnp.dot(left, weight, preferred_element_type=jnp.float32)]
    ppermute x3 -> x0, waiting for transfers between devices: 40.1 us -> none  [exchange(): lax.ppermute(share, 'dp', [(i, i ^ step) for i in range(shares)])]
    another operation x2 -> x0, other arithmetic: 10.1 us -> none  [the longest x1 6.05 us: exchange(): return jnp.stack(ordered, axis=1).reshape(-1, share.shape[2])]
    convert_element_type x2 -> x0, other arithmetic: 5.14 us -> none  [the longest x1 3.01 us: on_device(): normed = layer_norm(resid_input, ln1_gain, ln1_bias).astype(jnp.bfloat16)]
    convert_element_type x1 -> x0, local copies, waits for them, and re-layouts: 4.23 us -> none  [on_device(): resid_input = flat_rows.astype(jnp.float32)]
    ppermute x3 -> x0, starting transfers between devices: 3.49 us -> none  [exchange(): lax.ppermute(share, 'dp', [(i, i ^ step) for i in range(shares)])]
  transfers between devices with their start and end apart: 7 -> 0, of which waited for: 5 -> 0; matrix products, arithmetic and copies ran while one was open for 17% -> 0% of each run, Pallas kernels for 11% -> 0%
where the time goes in v1:
time: 165 us; the launch traced here: 163 us
  Pallas kernels  151 us (92%)
  local copies, waits for them, and re-layouts  12.3 us (7%)
    pallas_call x1, Pallas kernels, fused(): pl.pallas_call(functools.partial(fused_kernel, plan), out_shape=jax.Shape...  151 us
    reshape x7, local copies, waits for them, and re-layouts, on_device(): return fused(plan, tokens, weights, [v.reshape(1, -1) for v in vectors])  9.1 us

profile of v1, /device:TPU:0, one launch (start us, length us, event | category | flops | bytes accessed | tf_op | source)
XLA Modules:
  0.0 163.3 jit_solution(17764035220973463774)
XLA Ops:
  0.0 1.3 reshape.24.ln1_gain
  1.3 1.3 reshape.25.ln1_bias
  2.6 1.3 reshape.27.proj_bias
  3.9 1.3 reshape.28.ln2_gain
  5.2 1.3 reshape.29.ln2_bias
  6.5 1.3 reshape.31.fc2_bias
  7.8 1.3 reshape.26.qkv_bias
  9.1 151.0 %shard_map.127 = bf16[3,257,1408]{2,1,0:T(8,128)(2,1)} custom-call(bf16[3,257,1408]{2,1,0:T(8,128)(2,1)} %tokens.1, bf16[176,4224]{1,0:T(8,128)(2,1)} %qkv_hbm.1, bf16[176,1408]{1,0:T(8,128)(2,1)} %proj_hbm.1, bf16[176,3072]{1,0:T(8,128)(2,1)} %fc1_hbm.1, bf16[384,1408]{1,0:T(8,128)(2,1)} %fc2_hbm.1, f32[1,1408]{1,0:T(1,128)} %reshape.24.ln1_gain, ...), custom_call_target="tpu_custom_call" | custom-call | tf_op jit(solution)/shard_map/pallas_call | solution.py:386
  160.1 3.2 %copy.15 = bf16[3,257,1408]{2,1,0:T(8,128)(2,1)} copy(bf16[3,257,1408]{2,1,0:T(8,128)(2,1)} %shard_map.127) | data formatting | bytes 4342272

commit v2 on v1

v2 whole, which is shorter than its diff:
```python
import functools
import math
import jax
import jax.numpy as jnp
from jax import lax
from jax.experimental import pallas as pl
from jax.experimental.pallas import tpu as pltpu
from jax.sharding import PartitionSpec as P

HEADS = 16
LANES = 128
PACK = 16
EPS = 1e-06
AHEAD = 2


def layer_norm(values, gain, bias):
    average = jnp.mean(values, axis=-1, keepdims=True)
    centered = values - average
    variance = jnp.mean(centered * centered, axis=-1, keepdims=True)
    return centered * lax.rsqrt(variance + EPS) * gain + bias


def product(left, weight):
    return jnp.dot(left, weight, preferred_element_type=jnp.float32)


def round_up(value, step):
    return -(-value // step) * step


def row_block(rows, most):
    best = PACK
    for size in range(PACK, most + 1, PACK):
        if rows % size == 0:
            best = size
    return best


class Plan:
    def __init__(self, shares, ring, tokens, weights):
        self.shares, self.ring = shares, ring
        self.images, self.seq, self.width = tokens.shape
        qkv, proj, fc1, fc2 = weights
        self.depth = qkv.shape[0]
        self.deep = fc2.shape[0]
        self.wide = [w.shape[1] for w in (qkv, proj, fc1)]
        self.total = sum(self.wide)
        self.chunk = shares * LANES
        self.hidden = fc1.shape[1]
        self.seq_pad = round_up(self.seq, PACK)
        self.rows = self.images * self.seq_pad
        zs = ring // 2
        self.fits = (
            shares == 4
            and ring % 2 == 0
            and zs >= 4
            and zs & (zs - 1) == 0
            and self.depth % PACK == 0
            and self.deep % (shares * PACK) == 0
            and all(w % LANES == 0 for w in self.wide)
            and self.total % self.chunk == 0
            and self.width % LANES == 0
            and self.width >= self.chunk
            and self.wide[0] == 3 * self.width
            and self.width % HEADS == 0
        )
        if not self.fits:
            return
        self.narrow = 2 * LANES
        self.col_chunks = self.total // self.chunk
        self.kinds = [("col", 0, self.col_chunks, self.chunk, 0)]
        whole = self.width // self.narrow
        at = self.col_chunks
        self.kinds.append(("row", at, at + whole, self.narrow, 0))
        at += whole
        if self.width % self.narrow:
            self.kinds.append(("row", at, at + 1, self.width % self.narrow, whole * self.narrow))
            at += 1
        self.chunks = at
        self.groups = self.width // self.chunk
        self.rest = self.width % self.chunk
        self.segments = []
        for group in range(self.groups):
            for piece in range(3):
                self.segments.append((0, piece * self.width + group * self.chunk, self.chunk))
        for piece in range(3):
            if self.rest:
                self.segments.append((0, piece * self.width + self.groups * self.chunk, self.rest))
        self.segments.append((1, 0, self.wide[1]))
        self.segments.append((2, 0, self.wide[2]))
        kept = ring * (self.depth * self.total + self.deep * self.width) * 2
        acts = self.rows * (self.width * (4 + 2 + 2 + 2) + max(3 * self.width, self.hidden) * 2)
        self.fits = kept + acts < 58 * 1024 * 1024


def flip(value, mask):
    bit = 1
    while bit <= mask:
        if mask & bit:
            value = value + bit - 2 * bit * lax.rem(value // bit, 2)
        bit *= 2
    return value


def fused_kernel(plan, tokens, qkv_hbm, proj_hbm, fc1_hbm, fc2_hbm,
                 ln1_gain, ln1_bias, qkv_bias, proj_bias, ln2_gain, ln2_bias, fc1_bias, fc2_bias,
                 out, wall, wtwo, tok, resid, normed, qkv, mixed,
                 send_sem, recv_sem, own_sem, out_sem):
    shares, ring = plan.shares, plan.ring
    zs = ring // 2
    depth, deep = plan.depth, plan.deep
    rows, seq, seq_pad = plan.rows, plan.seq, plan.seq_pad
    share = lax.axis_index("dp")
    place = lax.axis_index("fsdp")
    z, core = place // 2, lax.rem(place, 2)
    Z, X1, Y1, X2, Y2, PART = range(6)
    side_x, side_y, corner = flip(share, 1), flip(share, 2), flip(share, 3)
    partner = flip(place, 1)
    near = flip(z, 1) * 2 + core
    far = [flip(z, mask) * 2 + core for mask in range(2, zs)]

    def device(d, f):
        return {"dp": d, "fsdp": f}

    def part(kind, who, block_share):
        name, first, _, cols, base, g = kind
        if name == "col":
            r = pl.multiple_of(who * depth, PACK)
            c = pl.multiple_of((g * shares + block_share) * LANES, LANES)
            return wall.at[pl.ds(r, depth), pl.ds(c, LANES)]
        size = deep // shares
        r = pl.multiple_of(who * deep + block_share * size, PACK)
        c = pl.multiple_of(base + (g - first) * cols, LANES)
        return wtwo.at[pl.ds(r, size), pl.ds(c, cols)]

    def entire(kind, who):
        name, first, _, cols, base, g = kind
        if name == "col":
            return wall.at[pl.ds(pl.multiple_of(who * depth, PACK), depth),
                           pl.ds(pl.multiple_of(g * cols, LANES), cols)]
        return wtwo.at[pl.ds(pl.multiple_of(who * deep, PACK), deep),
                       pl.ds(pl.multiple_of(base + (g - first) * cols, LANES), cols)]

    def copy(ref, phase, g, d, f):
        return pltpu.make_async_remote_copy(
            src_ref=ref, dst_ref=ref, send_sem=send_sem.at[phase, g], recv_sem=recv_sem.at[phase, g],
            device_id=device(d, f), device_id_type=pl.DeviceIdType.MESH)

    def volume(kind, phase):
        name, cols = kind[0], kind[3]
        ref = wall if name == "col" else wtwo
        if phase == PART:
            return ref.at[pl.ds(0, zs * (depth if name == "col" else deep)), pl.ds(0, cols)]
        blocks = {Z: zs, X1: zs - 1, Y1: zs - 1, X2: (zs - 2) // 2, Y2: (zs - 2) // 2}[phase]
        size, cols = (depth, LANES) if name == "col" else (deep // shares, cols)
        return ref.at[pl.ds(0, blocks * size), pl.ds(0, cols)]

    def wait_on(kind, phase, sems):
        region = volume(kind, phase)
        pltpu.make_async_copy(region, region, sems.at[phase, kind[5]]).wait()

    def each_kind(g, body):
        if isinstance(g, int):
            for kind in plan.kinds:
                if kind[1] <= g < kind[2]:
                    body(kind + (g,))
            return
        for kind in plan.kinds:
            @pl.when(jnp.logical_and(g >= kind[1], g < kind[2]))
            def _(kind=kind):
                body(kind + (g,))

    def send_z(g):
        def body(kind):
            mine = part(kind, place, share)
            for other in far:
                copy(mine, Z, g, share, other).start()
            copy(mine, Z, g, share, near).start()
            copy(part(kind, place, corner), Z, g, share, near).start()
        each_kind(g, body)

    def relay_a(g):
        def body(kind):
            wait_on(kind, Z, recv_sem)
            for other in far + [near]:
                block = part(kind, other, share)
                copy(block, X1, g, side_x, place).start()
                copy(block, Y1, g, side_y, place).start()
        each_kind(g, body)

    def relay_b(g):
        def body(kind):
            wait_on(kind, X1, recv_sem)
            wait_on(kind, Y1, recv_sem)
            for one, two in zip(far[0::2], far[1::2]):
                copy(part(kind, one, side_y), X2, g, side_x, place).start()
                copy(part(kind, two, side_x), Y2, g, side_y, place).start()
        each_kind(g, body)

    def relay_c(g):
        def body(kind):
            wait_on(kind, X2, recv_sem)
            wait_on(kind, Y2, recv_sem)
            for who in [place, near] + far:
                copy(entire(kind, who), PART, g, share, partner).start()
        each_kind(g, body)

    def finish(g):
        each_kind(g, lambda kind: wait_on(kind, PART, recv_sem))

    ahead = AHEAD

    def tick(t):
        for low, action in ((ahead, send_z), (0, relay_a), (-1, relay_b), (-2, relay_c)):
            if not isinstance(t, int) or 0 <= t + low < plan.chunks:
                action(t + low)

    own = []
    base = 0
    for at, (which, low, size) in enumerate(plan.segments):
        ref = (qkv_hbm, proj_hbm, fc1_hbm)[which]
        own.append((which, pltpu.make_async_copy(
            ref.at[:, pl.ds(low, size)],
            wall.at[pl.ds(pl.multiple_of(place * depth, PACK), depth), pl.ds(base, size)],
            own_sem.at[at])))
        base += size
    own.append((3, pltpu.make_async_copy(
        fc2_hbm, wtwo.at[pl.ds(pl.multiple_of(place * deep, PACK), deep), :],
        own_sem.at[len(plan.segments)])))
    token_copy = pltpu.make_async_copy(tokens, tok, own_sem.at[len(plan.segments) + 1])
    barrier = pltpu.get_barrier_semaphore()
    peers = [(share, other) for other in far + [near, partner]]
    peers += [(side_x, place), (side_y, place)]
    for d, f in peers:
        pl.semaphore_signal(barrier, inc=1, device_id=device(d, f), device_id_type=pl.DeviceIdType.MESH)
    for which, c in own[:-3]:
        c.start()
    token_copy.start()
    for which, c in own[-3:]:
        c.start()
    pl.semaphore_wait(barrier, len(peers))
    for g in range(ahead):
        own[g][1].wait()
        send_z(g)

    token_copy.wait()
    for i in range(plan.images):
        tail = seq_pad - PACK
        resid[pl.ds(i * seq_pad + tail, PACK), :] = jnp.zeros((PACK, plan.width), jnp.float32)
        resid[pl.ds(i * seq_pad, seq), :] = tok[i].astype(jnp.float32)
    block = row_block(rows, 64)

    def norm(gain, bias):
        def body(r, carry):
            at = pl.ds(pl.multiple_of(r * block, PACK), block)
            normed[at, :] = layer_norm(resid[at, :], gain[...], bias[...]).astype(jnp.bfloat16)
            return carry
        lax.fori_loop(0, rows // block, body, 0)

    norm(ln1_gain, ln1_bias)
    for which, c in own[ahead:]:
        c.wait()

    cols = plan.chunk
    width = plan.width
    head_size = width // HEADS
    scale = head_size ** (-0.5) * math.log2(math.e)

    def project(source, target, size):
        source = pl.multiple_of(source, LANES)
        target = pl.multiple_of(target, LANES)
        qkv[:, pl.ds(target, size)] = (
            product(normed[...], wall[:, pl.ds(source, size)]) + qkv_bias[pl.ds(target, size)]
        ).astype(jnp.bfloat16)

    def project_chunk(g):
        project(g * cols, lax.rem(g, 3) * width + g // 3 * cols, cols)

    def attend(i, heads):
        at = pl.ds(pl.multiple_of(i * seq_pad, PACK), seq_pad)
        some = pl.ds(pl.multiple_of(i * seq_pad, PACK), seq)
        for head in heads:
            low = head * head_size
            q = qkv[at, low:low + head_size]
            k = qkv[some, width + low:width + low + head_size]
            v = qkv[some, 2 * width + low:2 * width + low + head_size]
            scores = lax.dot_general(q, k, (((1,), (1,)), ((), ())), preferred_element_type=jnp.float32)
            top = jnp.max(scores, axis=-1, keepdims=True)
            weights = jnp.exp2((scores - top) * scale)
            norm_by = 1.0 / jnp.sum(weights, axis=-1, keepdims=True)
            mixed[at, low:low + head_size] = (
                product(weights.astype(jnp.bfloat16), v) * norm_by).astype(jnp.bfloat16)

    ready = [0] + [(g + 1) * cols // head_size for g in range(plan.groups)] + [HEADS]
    heads_of = [list(range(low, high)) for low, high in zip(ready, ready[1:])]

    clock = [0]
    last_tick = plan.chunks + 2

    def advance(to):
        while clock[0] < to:
            tick(clock[0])
            clock[0] += 1

    advance(3)
    t = clock[0]

    def first_chunks(g, carry):
        tick(g + t)
        finish(g)
        project_chunk(g)
        return carry

    lax.fori_loop(0, 3, first_chunks, 0)
    clock[0] += 3
    for group in range(1, plan.groups):
        t = clock[0]

        def both(i, carry, group=group, t=t):
            attend(i, heads_of[group - 1])
            tick(t + i)
            finish(group * 3 + i)
            project_chunk(group * 3 + i)
            return carry

        fused_steps = min(3, plan.images)
        lax.fori_loop(0, fused_steps, both, 0)
        clock[0] += fused_steps
        for i in range(fused_steps, 3):
            advance(clock[0] + 1)
            finish(group * 3 + i)
            project_chunk(group * 3 + i)
        if plan.images > fused_steps:
            def more(i, carry, group=group):
                attend(i, heads_of[group - 1])
                return carry
            lax.fori_loop(fused_steps, plan.images, more, 0)
    t = clock[0]
    last_whole = heads_of[plan.groups - 1]

    def middle(i, carry):
        attend(i, last_whole)
        tick(t + i)
        return carry

    lax.fori_loop(0, plan.images, middle, 0)
    clock[0] += plan.images
    done = 3 * plan.groups

    def complete(columns):
        nonlocal done
        while done * cols < columns:
            advance(done + 3)
            finish(done)
            done += 1

    if plan.rest:
        complete(plan.wide[0])
        for piece in range(3):
            project(3 * plan.groups * cols + piece * plan.rest,
                    piece * width + plan.groups * cols, plan.rest)
        advance(clock[0] + 1)
    if heads_of[plan.groups]:
        t = clock[0]

        def last(i, carry):
            attend(i, heads_of[plan.groups])
            tick(t + i)
            return carry

        lax.fori_loop(0, plan.images, last, 0)
        clock[0] += plan.images

    at_proj = plan.wide[0]
    complete(plan.wide[0] + plan.wide[1])
    for low in range(0, width, 2 * LANES):
        high = min(low + 2 * LANES, width)
        resid[:, low:high] = (product(mixed[...], wall[:, at_proj + low:at_proj + high])
                              + proj_bias[low:high] + resid[:, low:high])
    advance(clock[0] + 1)
    norm(ln2_gain, ln2_bias)
    advance(clock[0] + 1)

    at_fc1 = plan.wide[0] + plan.wide[1]
    bounds = [at_fc1] + list(range(round_up(at_fc1 + 1, cols), plan.total + 1, cols))
    for count, (low, high) in enumerate(zip(bounds, bounds[1:])):
        complete(high)
        pre = product(normed[...], wall[:, low:high]) + fc1_bias[low - at_fc1:high - at_fc1]
        qkv[:, low - at_fc1:high - at_fc1] = (
            pre * (1.0 + lax.erf(pre * math.sqrt(0.5))) * 0.5).astype(jnp.bfloat16)
        if count % 2:
            advance(min(clock[0] + 1, last_tick))

    hidden = plan.hidden
    writes = []
    for g in range(plan.col_chunks, plan.chunks):
        advance(g + 3)
        finish(g)
        for kind in plan.kinds:
            if kind[1] <= g < kind[2]:
                low = kind[4] + (g - kind[1]) * kind[3]
                high = low + kind[3]
        for i in range(plan.images):
            at = slice(i * seq_pad, (i + 1) * seq_pad)
            down = product(qkv[at, :hidden], wtwo[:, low:high]) + fc2_bias[low:high] + resid[at, low:high]
            tok[i, :, low:high] = down.astype(jnp.bfloat16)[:seq]
            write = pltpu.make_async_copy(
                tok.at[i, :, pl.ds(low, high - low)], out.at[i, :, pl.ds(low, high - low)],
                out_sem.at[g - plan.col_chunks, i])
            write.start()
            writes.append(write)
        advance(min(clock[0] + 1, last_tick))
        if g == plan.chunks - 2:
            for phase in (Z, X1, Y1, X2, Y2, PART):
                def drain(g, carry, phase=phase):
                    each_kind(g, lambda kind: wait_on(kind, phase, send_sem))
                    return carry
                lax.fori_loop(0, plan.chunks, drain, 0)
    for write in writes:
        write.wait()


def fused(plan, tokens, weights, vectors):
    vmem = pl.BlockSpec(memory_space=pltpu.VMEM)
    anywhere = pl.BlockSpec(memory_space=pl.ANY)
    count = plan.chunks
    inner = max(plan.wide[0], plan.hidden)
    return pl.pallas_call(
        functools.partial(fused_kernel, plan),
        out_shape=jax.ShapeDtypeStruct(tokens.shape, jnp.bfloat16),
        in_specs=[anywhere] * 5 + [vmem] * len(vectors),
        out_specs=anywhere,
        scratch_shapes=[
            pltpu.VMEM((plan.ring * plan.depth, plan.total), jnp.bfloat16),
            pltpu.VMEM((plan.ring * plan.deep, plan.width), jnp.bfloat16),
            pltpu.VMEM(tokens.shape, jnp.bfloat16),
            pltpu.VMEM((plan.rows, plan.width), jnp.float32),
            pltpu.VMEM((plan.rows, plan.width), jnp.bfloat16),
            pltpu.VMEM((plan.rows, inner), jnp.bfloat16),
            pltpu.VMEM((plan.rows, plan.width), jnp.bfloat16),
            pltpu.SemaphoreType.DMA((6, count)),
            pltpu.SemaphoreType.DMA((6, count)),
            pltpu.SemaphoreType.DMA((len(plan.segments) + 2,)),
            pltpu.SemaphoreType.DMA((count - plan.col_chunks, plan.images)),
        ],
        compiler_params=pltpu.CompilerParams(
            collective_id=0, has_side_effects=True, vmem_limit_bytes=67_043_328),
    )(tokens, *weights, *vectors)


def gather(block):
    return lax.all_gather(block, "fsdp", axis=0, tiled=True)


def attend_kernel(head_size, q_ref, k_ref, v_ref, out_ref):
    scale = head_size ** (-0.5)
    for head in range(q_ref.shape[2] // head_size):
        at = slice(head * head_size, (head + 1) * head_size)
        scores = lax.dot_general(
            q_ref[0, :, at], k_ref[0, :, at], (((1,), (1,)), ((), ())),
            preferred_element_type=jnp.float32)
        top = jnp.max(scores, axis=-1, keepdims=True)
        weights = jnp.exp((scores - top) * scale)
        probs = weights / jnp.sum(weights, axis=-1, keepdims=True)
        mixed = product(probs.astype(jnp.bfloat16), v_ref[0, :, at])
        out_ref[0, :, at] = mixed.astype(jnp.bfloat16)


def attend(qkv, head_size):
    images, seq_len, wide = qkv.shape
    width = wide // 3
    spec = [
        pl.BlockSpec((1, seq_len, width), functools.partial(lambda part, i: (i, 0, part), part))
        for part in range(3)
    ]
    return pl.pallas_call(
        functools.partial(attend_kernel, head_size),
        grid=(images,),
        in_specs=spec,
        out_specs=pl.BlockSpec((1, seq_len, width), lambda i: (i, 0, 0)),
        out_shape=jax.ShapeDtypeStruct((images, seq_len, width), jnp.bfloat16),
        compiler_params=pltpu.CompilerParams(vmem_limit_bytes=48 * 1024 * 1024),
        cost_estimate=pl.CostEstimate(
            flops=4 * images * seq_len * seq_len * width,
            bytes_accessed=8 * images * seq_len * width,
            transcendentals=images * seq_len * seq_len * width // head_size,
        ),
    )(qkv, qkv, qkv)


def plain(tokens, ln1_gain, ln1_bias, qkv_weight, qkv_bias, proj_weight, proj_bias,
          ln2_gain, ln2_bias, fc1_weight, fc1_bias, fc2_weight, fc2_bias):
    images, seq_len, width = tokens.shape
    resid_input = tokens.reshape(-1, width).astype(jnp.float32)
    normed = layer_norm(resid_input, ln1_gain, ln1_bias).astype(jnp.bfloat16)
    qkv_sum = product(normed, gather(qkv_weight))
    qkv_proj = (qkv_sum + qkv_bias).astype(jnp.bfloat16).reshape(images, seq_len, 3 * width)
    attended = attend(qkv_proj, width // HEADS).reshape(-1, width)
    resid = product(attended, gather(proj_weight)) + proj_bias + resid_input
    normed_two = layer_norm(resid, ln2_gain, ln2_bias).astype(jnp.bfloat16)
    pre_act = product(normed_two, gather(fc1_weight))
    hidden = jax.nn.gelu(pre_act + fc1_bias, approximate=False).astype(jnp.bfloat16)
    result = product(hidden, gather(fc2_weight)) + fc2_bias + resid
    return result.astype(jnp.bfloat16).reshape(images, seq_len, width)


def on_device(tokens, ln1_gain, ln1_bias, qkv_weight, qkv_bias, proj_weight, proj_bias,
              ln2_gain, ln2_bias, fc1_weight, fc1_bias, fc2_weight, fc2_bias):
    weights = (qkv_weight, proj_weight, fc1_weight, fc2_weight)
    plan = Plan(lax.axis_size("dp"), lax.axis_size("fsdp"), tokens, weights)
    if not plan.fits:
        return plain(tokens, ln1_gain, ln1_bias, qkv_weight, qkv_bias, proj_weight, proj_bias,
                     ln2_gain, ln2_bias, fc1_weight, fc1_bias, fc2_weight, fc2_bias)
    vectors = (ln1_gain, ln1_bias, qkv_bias, proj_bias, ln2_gain, ln2_bias, fc1_bias, fc2_bias)
    return fused(plan, tokens, weights, vectors)


def solution(mesh):
    whole, rows = P(), P("fsdp", None)
    split = P(("dp", "fsdp"), None, None)
    placed = (split, whole, whole, rows, whole, rows, whole, whole, whole, rows, whole, rows, whole)
    return jax.shard_map(on_device, mesh=mesh, in_specs=placed, out_specs=split, check_vma=False)
```

time: 165 us -> 129 us (0.78)
  Pallas kernels: 151 us -> 125 us
  local copies, waits for them, and re-layouts: 12.3 us -> 3.16 us
    pallas_call x1, Pallas kernels: 151 us -> 125 us  [fused(): pl.pallas_call(functools.partial(fused_kernel, plan), out_shape=jax.Shape...]
    reshape x7 -> x0, local copies, waits for them, and re-layouts: 9.1 us -> none  [on_device(): return fused(plan, tokens, weights, [v.reshape(1, -1) for v in vectors])]
where the time goes in v2:
time: 129 us; the launch traced here: 128 us
  Pallas kernels  125 us (97%)
  local copies, waits for them, and re-layouts  3.16 us (2%)
    pallas_call x1, Pallas kernels, fused(): pl.pallas_call(functools.partial(fused_kernel, plan), out_shape=jax.Shape...  125 us
    unnamed x1, local copies, waits for them, and re-layouts  3.16 us

profile of v2, /device:TPU:0, one launch (start us, length us, event | category | flops | bytes accessed | tf_op | source)
XLA Modules:
  0.0 128.3 jit_solution(606097592586799890)
XLA Ops:
  0.0 125.2 %shard_map.127 = bf16[3,257,1408]{2,1,0:T(8,128)(2,1)} custom-call(bf16[3,257,1408]{2,1,0:T(8,128)(2,1)} %tokens.1, bf16[176,4224]{1,0:T(8,128)(2,1)} %qkv_hbm.1, bf16[176,1408]{1,0:T(8,128)(2,1)} %proj_hbm.1, bf16[176,3072]{1,0:T(8,128)(2,1)} %fc1_hbm.1, bf16[384,1408]{1,0:T(8,128)(2,1)} %fc2_hbm.1, f32[1408]{0:T(1024)} %ln1_gain.1, f32[1408]{0:T(1024)} %ln1_bias.1, ...), custom_call_target="tpu_custom_call" | custom-call | tf_op jit(solution)/shard_map/pallas_call | solution.py:429
  125.2 3.2 %copy.15 = bf16[3,257,1408]{2,1,0:T(8,128)(2,1)} copy(bf16[3,257,1408]{2,1,0:T(8,128)(2,1)} %shard_map.127) | data formatting | bytes 4342272

commit v3 on v2

--- a/solution.py
+++ b/solution.py
@@ -27,14 +27,6 @@
 
 def round_up(value, step):
     return -(-value // step) * step
-
-
-def row_block(rows, most):
-    best = PACK
-    for size in range(PACK, most + 1, PACK):
-        if rows % size == 0:
-            best = size
-    return best
 
 
 class Plan:
@@ -104,9 +96,10 @@
 
 
 def fused_kernel(plan, tokens, qkv_hbm, proj_hbm, fc1_hbm, fc2_hbm,
-                 ln1_gain, ln1_bias, qkv_bias, proj_bias, ln2_gain, ln2_bias, fc1_bias, fc2_bias,
-                 out, wall, wtwo, tok, resid, normed, qkv, mixed,
-                 send_sem, recv_sem, own_sem, out_sem):
+                 *rest):
+    vectors, out, held = rest[:8], rest[8], rest[9:17]
+    wall, wtwo, tok, resid, normed, qkv, mixed, send_sem, recv_sem, own_sem, out_sem, vec_sem = rest[17:]
+    ln1_gain, ln1_bias, qkv_bias, proj_bias, ln2_gain, ln2_bias, fc1_bias, fc2_bias = held
     shares, ring = plan.shares, plan.ring
     zs = ring // 2
     depth, deep = plan.depth, plan.deep
@@ -142,23 +135,33 @@
         return wtwo.at[pl.ds(pl.multiple_of(who * deep, PACK), deep),
                        pl.ds(pl.multiple_of(base + (g - first) * cols, LANES), cols)]
 
-    def copy(ref, phase, g, d, f):
+    def copy(ref, phase, kind, d, f):
+        g, form = kind[5], int(kind[0] == "row")
         return pltpu.make_async_remote_copy(
-            src_ref=ref, dst_ref=ref, send_sem=send_sem.at[phase, g], recv_sem=recv_sem.at[phase, g],
+            src_ref=ref, dst_ref=ref, send_sem=send_sem.at[phase, form], recv_sem=recv_sem.at[phase, g],
             device_id=device(d, f), device_id_type=pl.DeviceIdType.MESH)
+
+    blocks_of = {Z: zs, X1: zs - 1, Y1: zs - 1, X2: (zs - 2) // 2, Y2: (zs - 2) // 2}
 
     def volume(kind, phase):
         name, cols = kind[0], kind[3]
         ref = wall if name == "col" else wtwo
         if phase == PART:
             return ref.at[pl.ds(0, zs * (depth if name == "col" else deep)), pl.ds(0, cols)]
-        blocks = {Z: zs, X1: zs - 1, Y1: zs - 1, X2: (zs - 2) // 2, Y2: (zs - 2) // 2}[phase]
+        count = blocks_of[phase]
         size, cols = (depth, LANES) if name == "col" else (deep // shares, cols)
-        return ref.at[pl.ds(0, blocks * size), pl.ds(0, cols)]
-
-    def wait_on(kind, phase, sems):
+        return ref.at[pl.ds(0, count * size), pl.ds(0, cols)]
+
+    def totals(phase):
+        if phase == PART:
+            return wall.at[pl.ds(0, zs * depth), :], wtwo.at[pl.ds(0, zs * deep), :]
+        count = blocks_of[phase]
+        return (wall.at[pl.ds(0, count * depth), pl.ds(0, plan.col_chunks * LANES)],
+                wtwo.at[pl.ds(0, count * (deep // shares)), :])
+
+    def wait_on(kind, phase):
         region = volume(kind, phase)
-        pltpu.make_async_copy(region, region, sems.at[phase, kind[5]]).wait()
+        pltpu.make_async_copy(region, region, recv_sem.at[phase, kind[5]]).wait()
 
     def each_kind(g, body):
         if isinstance(g, int):
@@ -175,46 +178,56 @@
         def body(kind):
             mine = part(kind, place, share)
             for other in far:
-                copy(mine, Z, g, share, other).start()
-            copy(mine, Z, g, share, near).start()
-            copy(part(kind, place, corner), Z, g, share, near).start()
+                copy(mine, Z, kind, share, other).start()
+            copy(mine, Z, kind, share, near).start()
+            copy(part(kind, place, corner), Z, kind, share, near).start()
         each_kind(g, body)
 
     def relay_a(g):
         def body(kind):
-            wait_on(kind, Z, recv_sem)
+            wait_on(kind, Z)
             for other in far + [near]:
                 block = part(kind, other, share)
-                copy(block, X1, g, side_x, place).start()
-                copy(block, Y1, g, side_y, place).start()
+                copy(block, X1, kind, side_x, place).start()
+                copy(block, Y1, kind, side_y, place).start()
         each_kind(g, body)
 
     def relay_b(g):
         def body(kind):
-            wait_on(kind, X1, recv_sem)
-            wait_on(kind, Y1, recv_sem)
+            wait_on(kind, X1)
+            wait_on(kind, Y1)
             for one, two in zip(far[0::2], far[1::2]):
-                copy(part(kind, one, side_y), X2, g, side_x, place).start()
-                copy(part(kind, two, side_x), Y2, g, side_y, place).start()
+                copy(part(kind, one, side_y), X2, kind, side_x, place).start()
+                copy(part(kind, two, side_x), Y2, kind, side_y, place).start()
         each_kind(g, body)
 
     def relay_c(g):
         def body(kind):
-            wait_on(kind, X2, recv_sem)
-            wait_on(kind, Y2, recv_sem)
+            wait_on(kind, X2)
+            wait_on(kind, Y2)
             for who in [place, near] + far:
-                copy(entire(kind, who), PART, g, share, partner).start()
+                copy(entire(kind, who), PART, kind, share, partner).start()
         each_kind(g, body)
 
     def finish(g):
-        each_kind(g, lambda kind: wait_on(kind, PART, recv_sem))
+        each_kind(g, lambda kind: wait_on(kind, PART))
 
     ahead = AHEAD
 
-    def tick(t):
-        for low, action in ((ahead, send_z), (0, relay_a), (-1, relay_b), (-2, relay_c)):
+    def act(t, steps):
+        for low, action in steps:
             if not isinstance(t, int) or 0 <= t + low < plan.chunks:
                 action(t + low)
+
+    def tick_one(t):
+        act(t, ((ahead, send_z), (-3, relay_c), (0, relay_a)))
+
+    def tick_two(t):
+        act(t, ((-1, relay_b),))
+
+    def tick(t):
+        tick_one(t)
+        tick_two(t)
 
     own = []
     base = 0
@@ -234,10 +247,15 @@
     peers += [(side_x, place), (side_y, place)]
     for d, f in peers:
         pl.semaphore_signal(barrier, inc=1, device_id=device(d, f), device_id_type=pl.DeviceIdType.MESH)
-    for which, c in own[:-3]:
+    for which, c in own[:ahead]:
         c.start()
     token_copy.start()
-    for which, c in own[-3:]:
+    vector_copies = [
+        pltpu.make_async_copy(source, target, vec_sem.at[at])
+        for at, (source, target) in enumerate(zip(vectors, held))]
+    for c in vector_copies:
+        c.start()
+    for which, c in own[ahead:]:
         c.start()
     pl.semaphore_wait(barrier, len(peers))
     for g in range(ahead):
@@ -249,16 +267,19 @@
         tail = seq_pad - PACK
         resid[pl.ds(i * seq_pad + tail, PACK), :] = jnp.zeros((PACK, plan.width), jnp.float32)
         resid[pl.ds(i * seq_pad, seq), :] = tok[i].astype(jnp.float32)
-    block = row_block(rows, 64)
-
-    def norm(gain, bias):
+    block = seq_pad
+
+    def norm(gain, bias, low, high):
         def body(r, carry):
             at = pl.ds(pl.multiple_of(r * block, PACK), block)
             normed[at, :] = layer_norm(resid[at, :], gain[...], bias[...]).astype(jnp.bfloat16)
             return carry
-        lax.fori_loop(0, rows // block, body, 0)
-
-    norm(ln1_gain, ln1_bias)
+        lax.fori_loop(low, high, body, 0)
+
+    blocks = rows // block
+    for c in vector_copies:
+        c.wait()
+    norm(ln1_gain, ln1_bias, 0, blocks)
     for which, c in own[ahead:]:
         c.wait()
 
@@ -285,23 +306,39 @@
             q = qkv[at, low:low + head_size]
             k = qkv[some, width + low:width + low + head_size]
             v = qkv[some, 2 * width + low:2 * width + low + head_size]
-            scores = lax.dot_general(q, k, (((1,), (1,)), ((), ())), preferred_element_type=jnp.float32)
-            top = jnp.max(scores, axis=-1, keepdims=True)
+            scores = lax.dot_general(k, q, (((1,), (1,)), ((), ())), preferred_element_type=jnp.float32)
+            top = jnp.max(scores, axis=0, keepdims=True)
             weights = jnp.exp2((scores - top) * scale)
-            norm_by = 1.0 / jnp.sum(weights, axis=-1, keepdims=True)
-            mixed[at, low:low + head_size] = (
-                product(weights.astype(jnp.bfloat16), v) * norm_by).astype(jnp.bfloat16)
+            norm_by = 1.0 / jnp.sum(weights, axis=0, keepdims=True)
+            out_t = lax.dot_general(v, weights.astype(jnp.bfloat16), (((0,), (0,)), ((), ())),
+                                    preferred_element_type=jnp.float32) * norm_by
+            mixed[at, low:low + head_size] = out_t.T.astype(jnp.bfloat16)
+
+    def attend_ticking(i, heads, t):
+        tick_one(t)
+        attend(i, heads[:len(heads) // 2])
+        tick_two(t)
+        attend(i, heads[len(heads) // 2:])
 
     ready = [0] + [(g + 1) * cols // head_size for g in range(plan.groups)] + [HEADS]
     heads_of = [list(range(low, high)) for low, high in zip(ready, ready[1:])]
 
-    clock = [0]
-    last_tick = plan.chunks + 2
+    clock = [0, 0]
+    last_tick = plan.chunks + 3
+
+    def half():
+        if clock[0] < last_tick:
+            (tick_two if clock[1] else tick_one)(clock[0])
+            clock[0] += clock[1]
+            clock[1] = 1 - clock[1]
 
     def advance(to):
         while clock[0] < to:
-            tick(clock[0])
-            clock[0] += 1
+            half()
+
+    def reach(g):
+        while clock[0] < g + 3 or (clock[0] == g + 3 and not clock[1]):
+            half()
 
     advance(3)
     t = clock[0]
@@ -318,8 +355,9 @@
         t = clock[0]
 
         def both(i, carry, group=group, t=t):
+            tick_one(t + i)
             attend(i, heads_of[group - 1])
-            tick(t + i)
+            tick_two(t + i)
             finish(group * 3 + i)
             project_chunk(group * 3 + i)
             return carry
@@ -340,8 +378,7 @@
     last_whole = heads_of[plan.groups - 1]
 
     def middle(i, carry):
-        attend(i, last_whole)
-        tick(t + i)
+        attend_ticking(i, last_whole, t + i)
         return carry
 
     lax.fori_loop(0, plan.images, middle, 0)
@@ -351,7 +388,7 @@
     def complete(columns):
         nonlocal done
         while done * cols < columns:
-            advance(done + 3)
+            reach(done)
             finish(done)
             done += 1
 
@@ -360,13 +397,13 @@
         for piece in range(3):
             project(3 * plan.groups * cols + piece * plan.rest,
                     piece * width + plan.groups * cols, plan.rest)
-        advance(clock[0] + 1)
+            if piece < 2:
+                half()
     if heads_of[plan.groups]:
         t = clock[0]
 
         def last(i, carry):
-            attend(i, heads_of[plan.groups])
-            tick(t + i)
+            attend_ticking(i, heads_of[plan.groups], t + i)
             return carry
 
         lax.fori_loop(0, plan.images, last, 0)
@@ -374,13 +411,18 @@
 
     at_proj = plan.wide[0]
     complete(plan.wide[0] + plan.wide[1])
+    half()
     for low in range(0, width, 2 * LANES):
         high = min(low + 2 * LANES, width)
         resid[:, low:high] = (product(mixed[...], wall[:, at_proj + low:at_proj + high])
                               + proj_bias[low:high] + resid[:, low:high])
-    advance(clock[0] + 1)
-    norm(ln2_gain, ln2_bias)
-    advance(clock[0] + 1)
+        if low <= width // 2 < high:
+            half()
+    half()
+    norm(ln2_gain, ln2_bias, 0, blocks // 2)
+    half()
+    norm(ln2_gain, ln2_bias, blocks // 2, blocks)
+    half()
 
     at_fc1 = plan.wide[0] + plan.wide[1]
     bounds = [at_fc1] + list(range(round_up(at_fc1 + 1, cols), plan.total + 1, cols))
@@ -389,18 +431,17 @@
         pre = product(normed[...], wall[:, low:high]) + fc1_bias[low - at_fc1:high - at_fc1]
         qkv[:, low - at_fc1:high - at_fc1] = (
             pre * (1.0 + lax.erf(pre * math.sqrt(0.5))) * 0.5).astype(jnp.bfloat16)
-        if count % 2:
-            advance(min(clock[0] + 1, last_tick))
+        half()
 
     hidden = plan.hidden
     writes = []
-    for g in range(plan.col_chunks, plan.chunks):
-        advance(g + 3)
-        finish(g)
-        for kind in plan.kinds:
-            if kind[1] <= g < kind[2]:
-                low = kind[4] + (g - kind[1]) * kind[3]
-                high = low + kind[3]
+    for g in range(plan.col_chunks, plan.chunks, 2):
+        final = min(g + 2, plan.chunks)
+        for each in range(g, final):
+            reach(each)
+            finish(each)
+        low = (g - plan.col_chunks) * plan.narrow
+        high = min(low + (final - g) * plan.narrow, width)
         for i in range(plan.images):
             at = slice(i * seq_pad, (i + 1) * seq_pad)
             down = product(qkv[at, :hidden], wtwo[:, low:high]) + fc2_bias[low:high] + resid[at, low:high]
@@ -410,28 +451,25 @@
                 out_sem.at[g - plan.col_chunks, i])
             write.start()
             writes.append(write)
-        advance(min(clock[0] + 1, last_tick))
-        if g == plan.chunks - 2:
+            half()
+        if final == plan.chunks:
             for phase in (Z, X1, Y1, X2, Y2, PART):
-                def drain(g, carry, phase=phase):
-                    each_kind(g, lambda kind: wait_on(kind, phase, send_sem))
-                    return carry
-                lax.fori_loop(0, plan.chunks, drain, 0)
+                for form, region in enumerate(totals(phase)):
+                    pltpu.make_async_copy(region, region, send_sem.at[phase, form]).wait()
     for write in writes:
         write.wait()
 
 
 def fused(plan, tokens, weights, vectors):
-    vmem = pl.BlockSpec(memory_space=pltpu.VMEM)
     anywhere = pl.BlockSpec(memory_space=pl.ANY)
     count = plan.chunks
     inner = max(plan.wide[0], plan.hidden)
     return pl.pallas_call(
         functools.partial(fused_kernel, plan),
         out_shape=jax.ShapeDtypeStruct(tokens.shape, jnp.bfloat16),
-        in_specs=[anywhere] * 5 + [vmem] * len(vectors),
+        in_specs=[anywhere] * (5 + len(vectors)),
         out_specs=anywhere,
-        scratch_shapes=[
+        scratch_shapes=[pltpu.VMEM(v.shape, v.dtype) for v in vectors] + [
             pltpu.VMEM((plan.ring * plan.depth, plan.total), jnp.bfloat16),
             pltpu.VMEM((plan.ring * plan.deep, plan.width), jnp.bfloat16),
             pltpu.VMEM(tokens.shape, jnp.bfloat16),
@@ -439,10 +477,11 @@
             pltpu.VMEM((plan.rows, plan.width), jnp.bfloat16),
             pltpu.VMEM((plan.rows, inner), jnp.bfloat16),
             pltpu.VMEM((plan.rows, plan.width), jnp.bfloat16),
-            pltpu.SemaphoreType.DMA((6, count)),
+            pltpu.SemaphoreType.DMA((6, 2)),
             pltpu.SemaphoreType.DMA((6, count)),
             pltpu.SemaphoreType.DMA((len(plan.segments) + 2,)),
             pltpu.SemaphoreType.DMA((count - plan.col_chunks, plan.images)),
+            pltpu.SemaphoreType.DMA((len(vectors),)),
         ],
         compiler_params=pltpu.CompilerParams(
             collective_id=0, has_side_effects=True, vmem_limit_bytes=67_043_328),

time: 129 us -> 117 us (0.907)
  Pallas kernels: 125 us -> 113 us
    pallas_call x1, Pallas kernels: 125 us -> 113 us  [fused(): pl.pallas_call(functools.partial(fused_kernel, plan), out_shape=jax.Shape...]
where the time goes in v3:
time: 117 us
  Pallas kernels  113 us (97%)
  local copies, waits for them, and re-layouts  3.16 us (3%)
    pallas_call x1, Pallas kernels, fused(): pl.pallas_call(functools.partial(fused_kernel, plan), out_shape=jax.Shape...  113 us
    unnamed x1, local copies, waits for them, and re-layouts  3.16 us

profile of v3, /device:TPU:0, one launch (start us, length us, event | category | flops | bytes accessed | tf_op | source)
XLA Modules:
  0.0 116.6 jit_solution(5925919354539200498)
XLA Ops:
  0.0 113.4 %shard_map.127 = bf16[3,257,1408]{2,1,0:T(8,128)(2,1)} custom-call(bf16[3,257,1408]{2,1,0:T(8,128)(2,1)} %tokens.1, bf16[176,4224]{1,0:T(8,128)(2,1)} %qkv_hbm.1, bf16[176,1408]{1,0:T(8,128)(2,1)} %proj_hbm.1, bf16[176,3072]{1,0:T(8,128)(2,1)} %fc1_hbm.1, bf16[384,1408]{1,0:T(8,128)(2,1)} %fc2_hbm.1, f32[1408]{0:T(1024)} %rest_0_.1, f32[1408]{0:T(1024)} %rest_1_.1, ...), custom_call_target="tpu_custom_call" | custom-call | tf_op jit(solution)/shard_map/pallas_call | solution.py:467
  113.4 3.2 %copy.15 = bf16[3,257,1408]{2,1,0:T(8,128)(2,1)} copy(bf16[3,257,1408]{2,1,0:T(8,128)(2,1)} %shard_map.127) | data formatting | bytes 4342272

commit v4 on v3

--- a/solution.py
+++ b/solution.py
@@ -435,8 +435,9 @@
 
     hidden = plan.hidden
     writes = []
-    for g in range(plan.col_chunks, plan.chunks, 2):
-        final = min(g + 2, plan.chunks)
+    starts = [g for g in range(plan.col_chunks, plan.chunks - 2, 2)]
+    starts += [g for g in range(plan.chunks - 2, plan.chunks) if g not in starts]
+    for g, final in zip(starts, starts[1:] + [plan.chunks]):
         for each in range(g, final):
             reach(each)
             finish(each)

time: 117 us -> 117 us (level)
  no operation moved by 1% of the time
where the time goes in v4:
time: 117 us
  Pallas kernels  114 us (97%)
  local copies, waits for them, and re-layouts  3.16 us (3%)
    pallas_call x1, Pallas kernels, fused(): pl.pallas_call(functools.partial(fused_kernel, plan), out_shape=jax.Shape...  114 us
    unnamed x1, local copies, waits for them, and re-layouts  3.16 us

profile of v4, /device:TPU:0, one launch (start us, length us, event | category | flops | bytes accessed | tf_op | source)
XLA Modules:
  0.0 116.9 jit_solution(15741672858242666699)
XLA Ops:
  0.0 113.7 %shard_map.127 = bf16[3,257,1408]{2,1,0:T(8,128)(2,1)} custom-call(bf16[3,257,1408]{2,1,0:T(8,128)(2,1)} %tokens.1, bf16[176,4224]{1,0:T(8,128)(2,1)} %qkv_hbm.1, bf16[176,1408]{1,0:T(8,128)(2,1)} %proj_hbm.1, bf16[176,3072]{1,0:T(8,128)(2,1)} %fc1_hbm.1, bf16[384,1408]{1,0:T(8,128)(2,1)} %fc2_hbm.1, f32[1408]{0:T(1024)} %rest_0_.1, f32[1408]{0:T(1024)} %rest_1_.1, ...), custom_call_target="tpu_custom_call" | custom-call | tf_op jit(solution)/shard_map/pallas_call | solution.py:468
  113.7 3.2 %copy.15 = bf16[3,257,1408]{2,1,0:T(8,128)(2,1)} copy(bf16[3,257,1408]{2,1,0:T(8,128)(2,1)} %shard_map.127) | data formatting | bytes 4342272
